TPU v7x, 32 devices: a whole 2x2x4 slice. The times are simulated.
32 devices in a mesh: pole: 4 (over x, core), row: 4 (over z), col: 2 (over y).
Axes of the slice: x: 2, y: 2, z: 4, core: 2. Of those that a mesh axis runs over, the one named last changes fastest.
Arguments:
- anc_inverse: bfloat16 [4, 2, 4, 192, 768], P('pole', None, None, 'col', 'row'), may hold values from -6 to 6
- panel: bfloat16 [4, 2, 768, 1024], P('pole', None, ('row', 'col')), may hold values from -0.21875 to 0.21875
- pattern: int32 [8, 2], replicated, may hold values 0 or 1
- diag_inverse: bfloat16 [4, 2, 1024, 512], P('pole', None, 'col', 'row'), may hold values from -6 to 6
- pole_weights: float32 [4, 2], P('pole'), may hold values from -4 to 4
Outputs:
- inv_panel: float32 [4, 2, 768, 1024], P('pole', None, 'row', 'col')
- inv_diag: bfloat16 [4, 2, 1024, 512], P('pole', None, 'col', 'row')
- density: float32 [1024, 512], P('col', 'row')
All inputs are finite; a program needn't handle non-finite values.
Results may differ from a plain program's by a relative error of at most 0.013.
Values may be sent and summed in bfloat16 or wider, within the bound.
A program may use at most 128 MiB of HBM per device.

v0:
```python
import jax
import jax.numpy as jnp
from jax import lax
from jax.sharding import PartitionSpec as P


def complex_left(left_re, left_im, right_re, right_im):
    upper = jnp.concatenate([left_re, left_im], axis=1)
    lower = jnp.concatenate([-left_im, left_re], axis=1)
    left_side = jnp.concatenate([upper, lower], axis=0)
    right_side = jnp.concatenate([right_re, right_im], axis=0)
    product = lax.dot_general(
        left_side, right_side, (((0,), (0,)), ((), ())), preferred_element_type=jnp.float32
    )
    return product.reshape(2, left_re.shape[1], right_re.shape[1])


def body(anc_inverse, panel, pattern, diag_inverse, pole_weights):
    n_row = lax.axis_size("row")
    n_col = lax.axis_size("col")
    fine_block = lax.axis_index("row") * n_col + lax.axis_index("col")
    pattern_row = lax.dynamic_slice_in_dim(pattern, fine_block, 1, 0)
    block_rows = panel.shape[2]
    width_all = panel.shape[3]
    groups = pattern.shape[1]
    keep_mask = pattern_row.astype(jnp.bfloat16).reshape(1, 1, 1, groups, 1)
    masked = (panel.reshape(1, 2, block_rows, groups, width_all // groups) * keep_mask).reshape(
        1, 2, block_rows, width_all
    )
    local_rows = lax.all_to_all(masked, "col", split_axis=3, concat_axis=2, tiled=True)
    row_count = anc_inverse.shape[4]
    col_count = local_rows.shape[3]
    full_cols = lax.all_gather(local_rows, "row", axis=2, tiled=True)
    stacked = full_cols[0].reshape(2, n_row, block_rows * n_col, col_count)
    segment = lax.all_gather(anc_inverse, "col", axis=3, tiled=True)
    length = segment.shape[3]
    left_side = segment[0].reshape(2, n_row * length, row_count)
    right_side = stacked.reshape(2, n_row * length, col_count)
    summed = complex_left(left_side[0], left_side[1], right_side[0], right_side[1])
    result_panel = -summed
    rounded = result_panel.astype(jnp.bfloat16)
    diag_terms = complex_left(local_rows[0, 0], local_rows[0, 1], rounded[0], rounded[1])
    row_share = lax.psum_scatter(diag_terms, "row", scatter_dimension=2, tiled=True)
    inverse_diag = diag_inverse[0].astype(jnp.float32) - row_share
    pole_weight = pole_weights[0]
    density_term = pole_weight[0] * inverse_diag[1] + pole_weight[1] * inverse_diag[0]
    density = lax.psum(density_term.astype(jnp.bfloat16), "pole").astype(jnp.float32)
    return (result_panel[None], inverse_diag.astype(jnp.bfloat16)[None], density)


def solution(mesh):
    placed = (
        P("pole", None, None, "col", "row"),
        P("pole", None, ("row", "col"), None),
        P(),
        P("pole", None, "col", "row"),
        P("pole", None),
    )
    return jax.shard_map(
        body,
        mesh=mesh,
        in_specs=placed,
        out_specs=(P("pole", None, "row", "col"), P("pole", None, "col", "row"), P("col", "row")),
        check_vma=False,
    )
```

profile of v0, /device:TPU:0, one launch (start us, length us, event | category | flops | bytes accessed | tf_op | source)
XLA Modules:
  0.0 151.4 jit_solution(4732061525736366362)
XLA Ops:
  7.2 0.0 all-gather.2.cloned.1.call-start
  7.2 0.9 fusion.26
  8.1 0.1 broadcast_bitcast_fusion
  8.2 1.0 broadcast_multiply_fusion
  9.2 0.4 copy.12
  9.6 0.0 copy-start.1
  9.6 12.2 %all_to_all.18 = bf16[1,2,96,1024]{2,1,0,3:T(2,128)(2,1)S(1)} all-to-all(bf16[1,2,96,1024]{2,1,0,3:T(2,128)(2,1)S(1)} %copy.12), channel_id=1, replica_groups=mesh['pole'=4,'row'=4,'col'=2] {'col'}, dimensions={3} | all-to-all | bytes 786432 | tf_op jit(solution)/shard_map/all_to_all | solution.py:30
  21.8 0.8 copy.15
  22.6 0.8 copy.14
  23.4 0.0 all-gather.2.cloned.1.call-update
  23.4 0.0 copy-start
  23.4 0.0 reduce-scatter.2.cloned.1.call-start
  23.5 0.0 copy-done.1
  23.5 10.5 %all_gather.6 = bf16[1,2,4,192,192]{4,3,2,1,0:T(8,128)(2,1)S(1)} all-gather(bf16[1,2,4,96,192]{4,3,2,1,0:T(8,128)(2,1)S(1)} %copy-done.1), channel_id=1, replica_groups=mesh['pole'=4,'row'=4,'col'=2] {'col'}, dimensions={3}, use_global_device_ids=true | all-gather | bytes 884736 | tf_op jit(solution)/shard_map/all_gather | solution.py:35
  34.0 0.1 fusion.30
  34.1 0.1 bitcast_negate_fusion
  34.1 0.0 copy-done
  34.2 26.8 %all-gather.2.cloned.1.call-done = bf16[1,2,768,512]{3,2,1,0:T(8,128)(2,1)} async-done(((bf16[1,2,192,512]{3,2,1,0:T(8,128)(2,1)}), bf16[1,2,768,512]{3,2,1,0:T(8,128)(2,1)}) %all-gather.2.cloned.1.call-update) | async-done | bytes 1572880 | tf_op jit(solution)/shard_map/all_gather | solution.py:33
  61.0 1.5 slice_bitcast_fusion.1
  62.5 1.1 fusion.4
  63.6 0.0 copy-start.4
  63.6 2.1 %fusion.14 = f32[1024,512]{1,0:T(8,128)} fusion(bf16[192,512]{1,0:T(8,128)(2,1)S(1)} %get-tuple-element.10, bf16[192,512]{1,0:T(8,128)(2,1)S(1)} %fusion.29, bf16[192,512]{1,0:T(8,128)(2,1)S(1)} %get-tuple-element.9, f32[384,512]{1,0:T(8,128)S(1)} %fusion.4), kind=kOutput, calls=%fused_computation.14 | convolution fusion | flops 405995520 | bytes 3473408 | tf_op jit(solution)/shard_map/dot_general | solution.py:12
  65.7 0.0 copy-done.4
  65.7 0.0 copy-start.3
  65.7 0.0 copy-start.2
  65.7 0.0 reduce-scatter.2.cloned.1.call-update
  65.7 0.0 all-reduce.2.cloned.1.call-start
  65.8 0.6 copy-done.3
  66.3 0.6 fusion.31
  67.0 41.4 %reduce-scatter.2.cloned.1.call-done = f32[2,512,128]{2,1,0:T(8,128)} async-done(((f32[2,512,512]{2,1,0:T(8,128)}), f32[2,512,128]{2,1,0:T(8,128)}) %reduce-scatter.2.cloned.1.call-update) | async-done | bytes 524304 | tf_op jit(solution)/shard_map/reduce_scatter | solution.py:43
  108.4 0.0 copy-done.2
  108.4 1.8 %convert_bitcast_fusion = (bf16[1,2,512,128]{3,2,1,0:T(8,128)(2,1)}, f32[2,512,128]{2,1,0:T(8,128)S(1)}) fusion(f32[2,512,128]{2,1,0:T(8,128)} %reduce-scatter.2.cloned.1.call-done, bf16[1,2,512,128]{3,2,1,0:T(8,128)(2,1)S(1)} %copy-done.2), kind=kLoop, calls=%fused_computation.28 | loop fusion | flops 393216 | bytes 1572864 | tf_op jit(solution)/shard_map/broadcast_in_dim | solution.py:48
  110.2 1.9 %fusion.25 = bf16[512,128]{1,0:T(8,128)(2,1)} fusion(f32[2,512,128]{2,1,0:T(8,128)S(1)} %get-tuple-element.4, f32[]{:T(128)} %bitcast.14, f32[]{:T(128)} %bitcast.13), kind=kLoop, calls=%fused_computation.32 | loop fusion | flops 262144 | bytes 655368 | tf_op jit(solution)/shard_map/convert_element_type | solution.py:47
  112.1 0.0 all-reduce.2.cloned.1.call-update
  112.1 31.1 %all-reduce.2.cloned.1.call-done = bf16[512,128]{1,0:T(8,128)(2,1)} async-done(((bf16[512,128]{1,0:T(8,128)(2,1)}), bf16[512,128]{1,0:T(8,128)(2,1)}) %all-reduce.2.cloned.1.call-update) | async-done | bytes 131088 | tf_op jit(solution)/shard_map/psum | solution.py:47
  143.2 1.6 %convert_element_type.32 = f32[512,128]{1,0:T(8,128)} convert(bf16[512,128]{1,0:T(8,128)(2,1)} %all-reduce.2.cloned.1.call-done) | non-fusion elementwise | flops 65536 | bytes 393216 | tf_op jit(solution)/shard_map/convert_element_type | solution.py:47
  (3 shorter events, 0.1 us)
Async XLA Ops:
  7.2 53.8 %all-gather.2.cloned.1.call-start = ((), (), s32[]{:S(2)}) async-start(), calls=%async_computation.2 | async-start | bytes 1966080 | tf_op jit(solution)/shard_map/all_gather | solution.py:33
  9.6 13.9 %copy-start.1 = (bf16[1,2,4,96,192]{4,3,2,1,0:T(8,128)(2,1)S(1)}, bf16[1,2,4,96,192]{4,3,2,1,0:T(8,128)(2,1)}, u32[]{:S(2)}) copy-start(bf16[1,2,4,96,192]{4,3,2,1,0:T(8,128)(2,1)} %param.5) | copy-start | bytes 884740
  23.4 10.7 %copy-start = (bf16[1,2,2,96,512]{4,3,2,1,0:T(8,128)(2,1)S(1)}, bf16[1,2,2,96,512]{4,3,2,1,0:T(8,128)(2,1)}, u32[]{:S(2)}) copy-start(bf16[1,2,2,96,512]{4,3,2,1,0:T(8,128)(2,1)} %copy.14) | copy-start | bytes 1179652
  23.4 84.9 %reduce-scatter.2.cloned.1.call-start = ((), (), s32[]{:S(2)}) async-start(), calls=%async_computation.3 | async-start | bytes 2621440 | tf_op jit(solution)/shard_map/reduce_scatter | solution.py:43
  63.6 2.1 %copy-start.4 = (f32[384,512]{1,0:T(8,128)}, f32[384,512]{1,0:T(8,128)S(1)}, u32[]{:S(2)}) copy-start(f32[384,512]{1,0:T(8,128)S(1)} %fusion.4) | copy-start | bytes 2359300
  65.7 0.7 copy-start.3
  65.7 42.7 %copy-start.2 = (bf16[1,2,512,128]{3,2,1,0:T(8,128)(2,1)S(1)}, bf16[1,2,512,128]{3,2,1,0:T(8,128)(2,1)}, u32[]{:S(2)}) copy-start(bf16[1,2,512,128]{3,2,1,0:T(8,128)(2,1)} %param.8) | copy-start | bytes 786436
  65.7 77.5 %all-reduce.2.cloned.1.call-start = ((), (), s32[]{:S(2)}) async-start(), calls=%async_computation.4 | async-start | bytes 262144 | tf_op jit(solution)/shard_map/psum | solution.py:47
Sparse Core Ops, SparseCore 0:
  23.5 37.4 all-gather.1
  65.8 42.5 reduce-scatter.1
  112.2 30.9 all-reduce.1
where the time goes:
time: 152 us; the launch traced here: 151 us
  waiting for transfers between devices  99.4 us (65%)
  blocking collectives  22.7 us (15%)
  between operations  13.8 us (9%)
  other arithmetic  7.29 us (5%)
  local copies, waits for them, and re-layouts  4.86 us (3%)
  matrix products  3.19 us (2%)
    reduce_scatter x1, waiting for transfers between devices, body(): lax.psum_scatter(diag_terms, 'row', scatter_dimension=2, tiled=True)  41.4 us
    psum x1, waiting for transfers between devices, body(): lax.psum(density_term.astype(jnp.bfloat16), 'pole').astype(jnp.float32)  31.1 us
    all_gather x1, waiting for transfers between devices, body(): full_cols = lax.all_gather(local_rows, 'row', axis=2, tiled=True)  26.8 us
    all_to_all x1, blocking collectives, body(): lax.all_to_all(masked, 'col', split_axis=3, concat_axis=2, tiled=True)  12.2 us
    all_gather x1, blocking collectives, body(): segment = lax.all_gather(anc_inverse, 'col', axis=3, tiled=True)  10.5 us
    dot_general x2, matrix products, complex_left(): lax.dot_general(left_side, right_side, (((0,), (0,)), ((), ())), preferre...  3.19 us
  transfers between devices with their start and end apart: 3, of which 3 were waited for; matrix products, arithmetic and copies ran while one was open for 1% of the time, Pallas kernels for 0%

commit v1 on v0

--- a/solution.py
+++ b/solution.py
@@ -44,7 +44,9 @@
     inverse_diag = diag_inverse[0].astype(jnp.float32) - row_share
     pole_weight = pole_weights[0]
     density_term = pole_weight[0] * inverse_diag[1] + pole_weight[1] * inverse_diag[0]
-    density = lax.psum(density_term.astype(jnp.bfloat16), "pole").astype(jnp.float32)
+    density = jnp.sum(lax.all_gather(density_term.astype(jnp.bfloat16), "pole"), axis=0).astype(
+        jnp.float32
+    )
     return (result_panel[None], inverse_diag.astype(jnp.bfloat16)[None], density)
 
 

time: 152 us -> 127 us (0.84)
  waiting for transfers between devices: 99.4 us -> 68.2 us
  blocking collectives: 22.7 us -> 29.8 us
    psum x1 -> x0, waiting for transfers between devices: 31.1 us -> none  [body(): lax.psum(density_term.astype(jnp.bfloat16), 'pole').astype(jnp.float32)]
    all_gather x0 -> x1, blocking collectives: none -> 7.13 us  [body(): lax.all_gather(density_term.astype(jnp.bfloat16), 'pole')]
  transfers between devices with their start and end apart: 3 -> 2, of which waited for: 3 -> 2; matrix products, arithmetic and copies ran while one was open for 1% -> 1% of each run, Pallas kernels for 0% -> 0%
where the time goes in v1:
time: 127 us; the launch traced here: 126 us
  waiting for transfers between devices  68.2 us (54%)
  blocking collectives  29.8 us (23%)
  between operations  14.2 us (11%)
  other arithmetic  5.94 us (5%)
  local copies, waits for them, and re-layouts  4.94 us (4%)
  matrix products  3.2 us (3%)
    reduce_scatter x1, waiting for transfers between devices, body(): lax.psum_scatter(diag_terms, 'row', scatter_dimension=2, tiled=True)  41.4 us
    all_gather x1, waiting for transfers between devices, body(): full_cols = lax.all_gather(local_rows, 'row', axis=2, tiled=True)  26.8 us
    all_to_all x1, blocking collectives, body(): lax.all_to_all(masked, 'col', split_axis=3, concat_axis=2, tiled=True)  12.2 us
    all_gather x1, blocking collectives, body(): segment = lax.all_gather(anc_inverse, 'col', axis=3, tiled=True)  10.5 us
    all_gather x1, blocking collectives, body(): lax.all_gather(density_term.astype(jnp.bfloat16), 'pole')  7.13 us
    dot_general x2, matrix products, complex_left(): lax.dot_general(left_side, right_side, (((0,), (0,)), ((), ())), preferre...  3.2 us
  transfers between devices with their start and end apart: 2, of which 2 were waited for; matrix products, arithmetic and copies ran while one was open for 1% of the time, Pallas kernels for 0%

profile of v1, /device:TPU:0, one launch (start us, length us, event | category | flops | bytes accessed | tf_op | source)
XLA Modules:
  0.0 126.3 jit_solution(17357969155942034795)
XLA Ops:
  7.2 0.0 all-gather.2.cloned.1.call-start
  7.2 0.9 fusion.25
  8.1 0.1 broadcast_bitcast_fusion
  8.2 1.0 broadcast_multiply_fusion
  9.2 0.4 copy.12
  9.6 0.0 copy-start.1
  9.6 12.2 %all_to_all.18 = bf16[1,2,96,1024]{2,1,0,3:T(2,128)(2,1)S(1)} all-to-all(bf16[1,2,96,1024]{2,1,0,3:T(2,128)(2,1)S(1)} %copy.12), channel_id=1, replica_groups=mesh['pole'=4,'row'=4,'col'=2] {'col'}, dimensions={3} | all-to-all | bytes 786432 | tf_op jit(solution)/shard_map/all_to_all | solution.py:30
  21.8 0.8 copy.15
  22.6 0.8 copy.14
  23.4 0.0 all-gather.2.cloned.1.call-update
  23.4 0.0 copy-start
  23.4 0.0 reduce-scatter.2.cloned.1.call-start
  23.5 0.0 copy-done.1
  23.5 10.5 %all_gather.10 = bf16[1,2,4,192,192]{4,3,2,1,0:T(8,128)(2,1)S(1)} all-gather(bf16[1,2,4,96,192]{4,3,2,1,0:T(8,128)(2,1)S(1)} %copy-done.1), channel_id=1, replica_groups=mesh['pole'=4,'row'=4,'col'=2] {'col'}, dimensions={3}, use_global_device_ids=true | all-gather | bytes 884736 | tf_op jit(solution)/shard_map/all_gather | solution.py:35
  34.0 0.1 fusion.29
  34.1 0.1 bitcast_negate_fusion
  34.1 0.0 copy-done
  34.2 26.8 %all-gather.2.cloned.1.call-done = bf16[1,2,768,512]{3,2,1,0:T(8,128)(2,1)} async-done(((bf16[1,2,192,512]{3,2,1,0:T(8,128)(2,1)}), bf16[1,2,768,512]{3,2,1,0:T(8,128)(2,1)}) %all-gather.2.cloned.1.call-update) | async-done | bytes 1572880 | tf_op jit(solution)/shard_map/all_gather | solution.py:33
  61.0 1.5 %slice_bitcast_fusion.1 = (bf16[768,512]{1,0:T(8,128)(2,1)S(1)}, bf16[768,512]{1,0:T(8,128)(2,1)S(1)}) fusion(bf16[1,2,768,512]{3,2,1,0:T(8,128)(2,1)} %all-gather.2.cloned.1.call-done), kind=kLoop, calls=%fused_computation.13 | loop fusion | bytes 3145728 | tf_op jit(solution)/shard_map/squeeze | solution.py:39
  62.5 1.1 fusion.4
  63.6 0.0 copy-start.4
  63.6 2.1 %fusion.14 = f32[1024,512]{1,0:T(8,128)} fusion(bf16[192,512]{1,0:T(8,128)(2,1)S(1)} %get-tuple-element.10, bf16[192,512]{1,0:T(8,128)(2,1)S(1)} %fusion.28, bf16[192,512]{1,0:T(8,128)(2,1)S(1)} %get-tuple-element.9, f32[384,512]{1,0:T(8,128)S(1)} %fusion.4), kind=kOutput, calls=%fused_computation.14 | convolution fusion | flops 405995520 | bytes 3473408 | tf_op jit(solution)/shard_map/dot_general | solution.py:12
  65.7 0.0 copy-done.4
  65.7 0.0 copy-start.3
  65.7 0.0 copy-start.2
  65.7 0.0 reduce-scatter.2.cloned.1.call-update
  65.7 0.6 copy-done.3
  66.4 0.6 fusion.30
  67.0 41.4 %reduce-scatter.2.cloned.1.call-done = f32[2,512,128]{2,1,0:T(8,128)} async-done(((f32[2,512,512]{2,1,0:T(8,128)}), f32[2,512,128]{2,1,0:T(8,128)}) %reduce-scatter.2.cloned.1.call-update) | async-done | bytes 524304 | tf_op jit(solution)/shard_map/reduce_scatter | solution.py:43
  108.4 0.0 copy-done.2
  108.4 1.8 %convert_bitcast_fusion = (bf16[1,2,512,128]{3,2,1,0:T(8,128)(2,1)}, f32[2,512,128]{2,1,0:T(8,128)S(1)}) fusion(f32[2,512,128]{2,1,0:T(8,128)} %reduce-scatter.2.cloned.1.call-done, bf16[1,2,512,128]{3,2,1,0:T(8,128)(2,1)S(1)} %copy-done.2), kind=kLoop, calls=%fused_computation.28 | loop fusion | flops 393216 | bytes 1572864 | tf_op jit(solution)/shard_map/broadcast_in_dim | solution.py:50
  110.2 1.4 %fusion.24 = bf16[1,512,128]{2,1,0:T(8,128)(2,1)S(1)} fusion(f32[2,512,128]{2,1,0:T(8,128)S(1)} %get-tuple-element.4, f32[]{:T(128)} %bitcast.14, f32[]{:T(128)} %bitcast.13), kind=kLoop, calls=%fused_computation.26 | loop fusion | flops 262144 | bytes 655368 | tf_op jit(solution)/shard_map/convert_element_type | solution.py:47
  111.6 7.1 %all_gather.12 = bf16[4,512,128]{2,1,0:T(8,128)(2,1)S(1)} all-gather(bf16[1,512,128]{2,1,0:T(8,128)(2,1)S(1)} %fusion.24), channel_id=1, replica_groups=mesh['pole'=4,'row'=4,'col'=2] {'pole'}, dimensions={0}, use_global_device_ids=true | all-gather | bytes 655360 | tf_op jit(solution)/shard_map/all_gather | solution.py:47
  118.7 0.1 reduce_sum.12
  118.8 0.7 convert_element_type.31
  (3 shorter events, 0.1 us)
Async XLA Ops:
  7.2 53.8 %all-gather.2.cloned.1.call-start = ((), (), s32[]{:S(2)}) async-start(), calls=%async_computation.2 | async-start | bytes 1966080 | tf_op jit(solution)/shard_map/all_gather | solution.py:33
  9.6 13.9 %copy-start.1 = (bf16[1,2,4,96,192]{4,3,2,1,0:T(8,128)(2,1)S(1)}, bf16[1,2,4,96,192]{4,3,2,1,0:T(8,128)(2,1)}, u32[]{:S(2)}) copy-start(bf16[1,2,4,96,192]{4,3,2,1,0:T(8,128)(2,1)} %param.5) | copy-start | bytes 884740
  23.4 10.7 %copy-start = (bf16[1,2,2,96,512]{4,3,2,1,0:T(8,128)(2,1)S(1)}, bf16[1,2,2,96,512]{4,3,2,1,0:T(8,128)(2,1)}, u32[]{:S(2)}) copy-start(bf16[1,2,2,96,512]{4,3,2,1,0:T(8,128)(2,1)} %copy.14) | copy-start | bytes 1179652
  23.4 85.0 %reduce-scatter.2.cloned.1.call-start = ((), (), s32[]{:S(2)}) async-start(), calls=%async_computation.3 | async-start | bytes 2621440 | tf_op jit(solution)/shard_map/reduce_scatter | solution.py:43
  63.6 2.1 %copy-start.4 = (f32[384,512]{1,0:T(8,128)}, f32[384,512]{1,0:T(8,128)S(1)}, u32[]{:S(2)}) copy-start(f32[384,512]{1,0:T(8,128)S(1)} %fusion.4) | copy-start | bytes 2359300
  65.7 0.7 copy-start.3
  65.7 42.7 %copy-start.2 = (bf16[1,2,512,128]{3,2,1,0:T(8,128)(2,1)S(1)}, bf16[1,2,512,128]{3,2,1,0:T(8,128)(2,1)}, u32[]{:S(2)}) copy-start(bf16[1,2,512,128]{3,2,1,0:T(8,128)(2,1)} %param.8) | copy-start | bytes 786436
Sparse Core Ops, SparseCore 0:
  23.5 37.4 all-gather.1
  65.9 42.5 reduce-scatter.1
